TPU v7x, 32 devices: a whole 2x2x4 slice. The times are simulated.
32 devices in a mesh: gx: 2 (over x), gy: 4 (over z), gz: 4 (over y, core).
Axes of the slice: x: 2, y: 2, z: 4, core: 2. Of those that a mesh axis runs over, the one named last changes fastest.
Arguments:
- pair_list: int32 [1024, 2], P(('gx', 'gy', 'gz')), may hold values from 0 to 63, all different within a row; in each aligned block of 32 rows (0 to 31, 32 to 63, ...) at most 2 rows name the same one
- rank_bucket: int32 [1024], P(('gx', 'gy', 'gz')), may hold values from 0 to 2
- amplitudes: bfloat16 [1024, 36864], P(('gx', 'gy', 'gz')), may hold values from -0.4375 to 0.4375
- intersects: bfloat16 [1024, 36864], P(('gx', 'gy', 'gz')), may hold values from -0.4375 to 0.4375
- integrals: bfloat16 [1024, 36864], P(('gx', 'gy', 'gz')), may hold values from -6 to 6
- exchange_blocks: bfloat16 [64, 36864], P(('gx', 'gy')), may hold values from -0.4375 to 0.4375
Outputs:
- residuals: bfloat16 [1024, 36864], P(('gx', 'gy', 'gz'))
Inputs may be any that keep to these rules, and one draw needn't show every extreme that they name: `pair_list`: each row names two different occupied orbitals; within the rows of one device no orbital is named more than 2 times, a bound that some block reaches on some devices. `rank_bucket`: bucket b keeps the leading (b + 1) * 64 PNOs.
All inputs are finite; a program needn't handle non-finite values.
Results may differ from a plain program's by a relative error of at most 0.013.
Values may be sent and summed in bfloat16 or wider, within the bound.
A program may use at most 128 MiB of HBM per device.

v0:
```python
import jax
import jax.numpy as jnp
from jax import lax
from jax.sharding import PartitionSpec as P

RSTEP = 64
R = 192


def body(pair_list, rank_bucket, amplitudes, intersects, integrals, exchange_blocks):
    pair_rows = amplitudes.shape[0]
    rank_width = R
    owned_rows = exchange_blocks.shape[0]
    amplitudes = amplitudes.reshape(pair_rows, rank_width, rank_width)
    intersects = intersects.reshape(pair_rows, rank_width, rank_width)
    integrals = integrals.reshape(pair_rows, rank_width, rank_width)
    exchange_blocks = exchange_blocks.reshape(owned_rows, rank_width, rank_width)
    groups_x, groups_y = (lax.axis_size("gx"), lax.axis_size("gy"))
    group_total = groups_x * groups_y
    occupied = owned_rows * group_total
    row_index = lax.broadcasted_iota(jnp.int32, (rank_width, rank_width), 0)
    col_index = lax.broadcasted_iota(jnp.int32, (rank_width, rank_width), 1)
    pair_rank = (rank_bucket + 1) * RSTEP
    inside = (row_index[None] < pair_rank[:, None, None]) & (
        col_index[None] < pair_rank[:, None, None]
    )
    masked = jnp.where(inside, amplitudes, jnp.zeros_like(amplitudes))
    half_projected = jnp.einsum(
        "pab,pbc->pac", intersects, masked, preferred_element_type=jnp.float32
    ).astype(jnp.bfloat16)
    projected = jnp.einsum(
        "pab,pcb->pac", half_projected, intersects, preferred_element_type=jnp.float32
    ).astype(jnp.bfloat16)
    local_term = jnp.einsum("pab,pbc->pac", masked, integrals, preferred_element_type=jnp.float32)
    flat_projected = projected.reshape(pair_rows, rank_width * rank_width)
    end_counts = jnp.sum(
        (pair_list[None] == lax.broadcasted_iota(jnp.int32, (occupied, 1, 1), 0)).astype(jnp.int32),
        axis=2,
    ).astype(jnp.bfloat16)
    partial_sum = lax.psum_scatter(
        jnp.dot(end_counts, flat_projected, preferred_element_type=jnp.float32),
        ("gx", "gy"),
        scatter_dimension=0,
        tiled=True,
    ).reshape(owned_rows, rank_width, rank_width)
    domain = lax.psum(partial_sum, "gz")
    coupled = jnp.einsum(
        "oab,obc->oac",
        domain.astype(jnp.bfloat16),
        exchange_blocks,
        preferred_element_type=jnp.float32,
    ).astype(jnp.bfloat16)
    every_coupled, every_block = (
        lax.all_gather(coupled, ("gx", "gy"), axis=0, tiled=True),
        lax.all_gather(exchange_blocks, ("gx", "gy"), axis=0, tiled=True),
    )
    picked_blocks = every_block[pair_list]
    picked_coupled = every_coupled[pair_list]
    own_term = jnp.einsum(
        "pab,pebc->peac", projected, picked_blocks, preferred_element_type=jnp.float32
    ).astype(jnp.bfloat16)
    answers = (picked_coupled.astype(jnp.float32) - own_term.astype(jnp.float32)).astype(
        jnp.bfloat16
    )
    combined = (answers[:, 0].astype(jnp.float32) + answers[:, 1].astype(jnp.float32)).astype(
        jnp.bfloat16
    )
    half_back = jnp.einsum(
        "pba,pbc->pac", intersects, combined, preferred_element_type=jnp.float32
    ).astype(jnp.bfloat16)
    back_projected = jnp.einsum(
        "pab,pbc->pac", half_back, intersects, preferred_element_type=jnp.float32
    )
    residual_sum = integrals.astype(jnp.float32) + local_term + back_projected
    result = jnp.where(inside, residual_sum, jnp.zeros_like(residual_sum)).astype(jnp.bfloat16)
    return result.reshape(pair_rows, rank_width * rank_width)


def solution(mesh):
    placed = (
        P(("gx", "gy", "gz"), None),
        P(("gx", "gy", "gz")),
        P(("gx", "gy", "gz"), None),
        P(("gx", "gy", "gz"), None),
        P(("gx", "gy", "gz"), None),
        P(("gx", "gy"), None),
    )
    return jax.shard_map(
        body, mesh=mesh, in_specs=placed, out_specs=P(("gx", "gy", "gz"), None), check_vma=False
    )
```

profile of v0, /device:TPU:0, one launch (start us, length us, event | category | flops | bytes accessed | tf_op | source)
XLA Modules:
  0.0 454.9 jit_solution(4188154951140406437)
XLA Ops:
  6.5 6.1 %reshape.28 = bf16[32,192,192]{2,1,0:T(8,128)(2,1)} reshape(bf16[32,36864]{1,0:T(8,128)(2,1)} %param.8) | data formatting | bytes 4718592 | tf_op jit(solution)/shard_map/reshape | solution.py:14
  12.7 5.0 %reshape.29 = bf16[32,192,192]{2,1,0:T(8,128)(2,1)S(1)} reshape(bf16[32,36864]{1,0:T(8,128)(2,1)} %param.9) | data formatting | bytes 4718592 | tf_op jit(solution)/shard_map/reshape | solution.py:15
  17.7 6.9 %fusion.19 = bf16[32,192,192]{2,1,0:T(8,128)(2,1)} fusion(bf16[32,192,192]{2,1,0:T(8,128)(2,1)S(1)} %reshape.29, bf16[32,192,192]{2,1,0:T(8,128)(2,1)} %reshape.28, s32[32]{0:T(128)S(1)} %add_multiply_fusion), kind=kOutput, calls=%fused_computation.20 | convolution fusion | flops 913047552 | bytes 7078016 | tf_op jit(solution)/shard_map/pab,pcb->pac/dot_general | solution.py:31
  24.5 6.2 %reshape.30 = bf16[32,36864]{1,0:T(8,128)(2,1)} reshape(bf16[32,192,192]{2,1,0:T(8,128)(2,1)} %fusion.19) | data formatting | bytes 4718592 | tf_op jit(solution)/shard_map/reshape | solution.py:35
  30.7 0.1 convert_reduce_fusion
  30.8 6.7 %fusion.26 = f32[64,36864]{1,0:T(8,128)} fusion(bf16[32,36864]{1,0:T(8,128)(2,1)} %reshape.30, s32[64,32]{0,1:T(8,128)S(1)} %convert_reduce_fusion), kind=kOutput, calls=%fused_computation.25 | convolution fusion | flops 150996992 | bytes 11804672 | tf_op jit(solution)/shard_map/dot_general | solution.py:41
  37.5 0.0 all-gather.5.cloned.1.call-start
  37.5 2.9 reshape.32
  40.5 162.0 %reduce-scatter.2.cloned.1.call-done = f32[8,36864]{1,0:T(8,128)} async-done(((f32[64,36864]{1,0:T(8,128)}), f32[8,36864]{1,0:T(8,128)}) %reduce-scatter.2.cloned.1.call-update) | async-done | bytes 1179664 | tf_op jit(solution)/shard_map/reduce_scatter | solution.py:40
  202.5 3.1 reshape.31
  205.6 34.0 %all-reduce.1 = bf16[8,192,192]{2,1,0:T(8,128)(2,1)} all-reduce(f32[8,192,192]{2,1,0:T(8,128)} %reshape.31), channel_id=1, replica_groups=mesh['gx'=2,'gy'=4,'gz'=4] {'gz'}, use_global_device_ids=true, to_apply=%region_2.3 | all-reduce | flops 294912 | bytes 1769472 | tf_op jit(solution)/shard_map/psum | solution.py:46
  239.6 2.6 convolution_convert_fusion
  242.2 0.1 copy.24
  242.3 0.1 reshape.36
  242.4 6.3 %reshape.27 = bf16[32,192,192]{2,1,0:T(8,128)(2,1)} reshape(bf16[32,36864]{1,0:T(8,128)(2,1)} %param.10) | data formatting | bytes 4718592 | tf_op jit(solution)/shard_map/reshape | solution.py:16
  248.7 53.7 %all-gather.5.cloned.1.call-done = bf16[64,192,192]{2,1,0:T(8,128)(2,1)} async-done(((bf16[8,192,192]{2,1,0:T(8,128)(2,1)}), bf16[64,192,192]{2,1,0:T(8,128)(2,1)}) %all-gather.5.cloned.1.call-update) | async-done | bytes 4718608 | tf_op jit(solution)/shard_map/all_gather | solution.py:55
  302.4 6.3 %gather_fusion.1 = bf16[64,192,192]{2,1,0:T(8,128)(2,1)} fusion(bf16[64,192,192]{2,1,0:T(8,128)(2,1)} %all-gather.5.cloned.1.call-done, s32[1024]{0:T(1024)S(1)} %pad_clamp_fusion), kind=kCustom, calls=%fused_computation.1 | custom fusion | bytes 9437440 | tf_op jit(solution)/shard_map/gather | solution.py:57
  308.7 92.7 %all-gather.3.cloned.1.call-done = bf16[64,192,192]{2,1,0:T(8,128)(2,1)} async-done(((bf16[8,192,192]{2,1,0:T(8,128)(2,1)}), bf16[64,192,192]{2,1,0:T(8,128)(2,1)}) %all-gather.3.cloned.1.call-update) | async-done | bytes 4718608 | tf_op jit(solution)/shard_map/all_gather | solution.py:54
  401.4 6.4 %gather_fusion = bf16[64,192,192]{2,1,0:T(8,128)(2,1)} fusion(bf16[64,192,192]{2,1,0:T(8,128)(2,1)} %all-gather.3.cloned.1.call-done, s32[1024]{0:T(1024)S(1)} %pad_clamp_fusion), kind=kCustom, calls=%fused_computation | custom fusion | bytes 9437440 | tf_op jit(solution)/shard_map/gather | solution.py:58
  407.9 9.7 %copy.25 = f32[64,192,192]{1,2,0:T(8,128)} copy(bf16[64,192,192]{2,1,0:T(8,128)(2,1)} %gather_fusion) | data formatting | bytes 14155776 | tf_op jit(solution)/shard_map/convert_element_type | solution.py:62
  417.5 11.3 %fusion = bf16[32,2,192,192]{2,3,1,0:T(8,128)(2,1)} fusion(f32[32,2,192,192]{2,3,1,0:T(8,128)} %bitcast.27, bf16[32,2,192,192]{3,2,1,0:T(8,128)(2,1)} %bitcast.28, bf16[32,192,192]{2,1,0:T(8,128)(2,1)} %fusion.19), kind=kOutput, calls=%fused_computation.3 | convolution fusion | flops 915406848 | bytes 21233664 | tf_op jit(solution)/shard_map/pab,pebc->peac/dot_general | solution.py:59
  428.8 7.5 %fusion.9 = f32[32,192,192]{2,1,0:T(8,128)} fusion(bf16[32,192,192]{2,1,0:T(8,128)(2,1)S(1)} %reshape.29, bf16[32,2,192,192]{2,3,1,0:T(8,128)(2,1)} %fusion), kind=kOutput, calls=%fused_computation.15 | convolution fusion | flops 911867904 | bytes 15728640 | tf_op jit(solution)/shard_map/pab,pbc->pac/dot_general | solution.py:71
  436.3 7.9 %select_convert_fusion = bf16[32,192,192]{2,1,0:T(8,128)(2,1)S(1)} fusion(f32[32,192,192]{2,1,0:T(8,128)} %fusion.9, bf16[32,192,192]{2,1,0:T(8,128)(2,1)} %reshape.27, s32[32]{0:T(128)S(1)} %add_multiply_fusion, bf16[32,192,192]{2,1,0:T(8,128)(2,1)} %reshape.28), kind=kOutput, calls=%fused_computation.4 | convolution fusion | flops 467140608 | bytes 11796608 | tf_op jit(solution)/shard_map/pab,pbc->pac/dot_general | solution.py:34
  444.1 4.2 reshape.33
  (12 shorter events, 0.1 us)
Async XLA Ops:
  6.5 195.9 %reduce-scatter.2.cloned.1.call-start = ((), (), s32[]{:S(2)}) async-start(), calls=%async_computation.1 | async-start | bytes 10616832 | tf_op jit(solution)/shard_map/reduce_scatter | solution.py:40
  12.7 5.0 %copy-start.1 = (s32[32]{0:T(128)S(1)}, s32[32]{0:T(128)}, u32[]{:S(2)}) copy-start(s32[32]{0:T(128)} %param.7) | copy-start | bytes 388
  24.5 6.2 %copy-start = (s32[32,2]{0,1:T(2,128)S(1)}, s32[32,2]{0,1:T(2,128)}, u32[]{:S(2)}) copy-start(s32[32,2]{0,1:T(2,128)} %param.6) | copy-start | bytes 772
  37.5 264.9 %all-gather.5.cloned.1.call-start = ((), (), s32[]{:S(2)}) async-start(), calls=%async_computation.3 | async-start | bytes 7077888 | tf_op jit(solution)/shard_map/all_gather | solution.py:55
  40.5 361.0 %all-gather.3.cloned.1.call-start = ((), (), s32[]{:S(2)}) async-start(), calls=%async_computation.2 | async-start | bytes 7077888 | tf_op jit(solution)/shard_map/all_gather | solution.py:54
Sparse Core Ops, SparseCore 0:
  37.6 164.8 reduce-scatter.1
  204.6 97.7 all-gather.4
  304.5 96.8 all-gather.2
where the time goes:
time: 456 us; the launch traced here: 455 us
  waiting for transfers between devices  308 us (68%)
  local copies, waits for them, and re-layouts  56.5 us (12%)
  matrix products  42.8 us (9%)
  blocking collectives  34 us (7%)
  between operations  13.2 us (3%)
    reduce_scatter x1, waiting for transfers between devices, body(): lax.psum_scatter(jnp.dot(end_counts, flat_projected, preferred_element_ty...  162 us
    all_gather x1, waiting for transfers between devices, body(): lax.all_gather(coupled, ('gx', 'gy'), axis=0, tiled=True)  92.7 us
    all_gather x1, waiting for transfers between devices, body(): lax.all_gather(exchange_blocks, ('gx', 'gy'), axis=0, tiled=True)  53.7 us
    psum x1, blocking collectives, body(): domain = lax.psum(partial_sum, 'gz')  34 us
    dot_general x1, matrix products, body(): jnp.einsum('pab,pebc->peac', projected, picked_blocks, preferred_element_...  11.3 us
    convert_element_type x1, local copies, waits for them, and re-layouts, body(): picked_coupled.astype(jnp.float32) - own_term.astype(jnp.float32)  9.66 us
  transfers between devices with their start and end apart: 3, of which 3 were waited for; matrix products, arithmetic and copies ran while one was open for 5% of the time, Pallas kernels for 0%

commit v1 on v0

--- a/solution.py
+++ b/solution.py
@@ -43,7 +43,7 @@
         scatter_dimension=0,
         tiled=True,
     ).reshape(owned_rows, rank_width, rank_width)
-    domain = lax.psum(partial_sum, "gz")
+    domain = jnp.sum(lax.all_gather(partial_sum, "gz"), axis=0)
     coupled = jnp.einsum(
         "oab,obc->oac",
         domain.astype(jnp.bfloat16),

time: 456 us -> 505 us (1.11)
  waiting for transfers between devices: 308 us -> 387 us
  blocking collectives: 34 us -> 0 us
    all_gather x0 -> x1, waiting for transfers between devices: none -> 42.4 us  [body(): domain = jnp.sum(lax.all_gather(partial_sum, 'gz'), axis=0)]
    psum x1 -> x0, blocking collectives: 34 us -> none  [body(): domain = lax.psum(partial_sum, 'gz')]
    all_gather x1, waiting for transfers between devices: 53.7 us -> 87.3 us  [body(): lax.all_gather(exchange_blocks, ('gx', 'gy'), axis=0, tiled=True)]
  transfers between devices with their start and end apart: 3 -> 4, of which waited for: 3 -> 4; matrix products, arithmetic and copies ran while one was open for 5% -> 5% of each run, Pallas kernels for 0% -> 0%
where the time goes in v1:
time: 505 us; the launch traced here: 504 us
  waiting for transfers between devices  387 us (77%)
  local copies, waits for them, and re-layouts  56.2 us (11%)
  matrix products  42.8 us (8%)
  between operations  13.2 us (3%)
    reduce_scatter x1, waiting for transfers between devices, body(): lax.psum_scatter(jnp.dot(end_counts, flat_projected, preferred_element_ty...  165 us
    all_gather x1, waiting for transfers between devices, body(): lax.all_gather(coupled, ('gx', 'gy'), axis=0, tiled=True)  92.5 us
    all_gather x1, waiting for transfers between devices, body(): lax.all_gather(exchange_blocks, ('gx', 'gy'), axis=0, tiled=True)  87.3 us
    all_gather x1, waiting for transfers between devices, body(): domain = jnp.sum(lax.all_gather(partial_sum, 'gz'), axis=0)  42.4 us
    dot_general x1, matrix products, body(): jnp.einsum('pab,pebc->peac', projected, picked_blocks, preferred_element_...  11.2 us
  transfers between devices with their start and end apart: 4, of which 4 were waited for; matrix products, arithmetic and copies ran while one was open for 5% of the time, Pallas kernels for 0%

profile of v1, /device:TPU:0, one launch (start us, length us, event | category | flops | bytes accessed | tf_op | source)
XLA Modules:
  0.0 504.3 jit_solution(6994494798054121088)
XLA Ops:
  6.5 6.1 %reshape.25 = bf16[32,192,192]{2,1,0:T(8,128)(2,1)} reshape(bf16[32,36864]{1,0:T(8,128)(2,1)} %param.8) | data formatting | bytes 4718592 | tf_op jit(solution)/shard_map/reshape | solution.py:14
  12.6 5.0 reshape.26
  17.6 6.9 %fusion.19 = bf16[32,192,192]{2,1,0:T(8,128)(2,1)} fusion(bf16[32,192,192]{2,1,0:T(8,128)(2,1)S(1)} %reshape.26, bf16[32,192,192]{2,1,0:T(8,128)(2,1)} %reshape.25, s32[32]{0:T(128)S(1)} %add_multiply_fusion), kind=kOutput, calls=%fused_computation.20 | convolution fusion | flops 913047552 | bytes 7078016 | tf_op jit(solution)/shard_map/pab,pcb->pac/dot_general | solution.py:31
  24.6 6.2 %reshape.27 = bf16[32,36864]{1,0:T(8,128)(2,1)} reshape(bf16[32,192,192]{2,1,0:T(8,128)(2,1)} %fusion.19) | data formatting | bytes 4718592 | tf_op jit(solution)/shard_map/reshape | solution.py:35
  30.8 6.7 %fusion.26 = f32[64,36864]{1,0:T(8,128)} fusion(bf16[32,36864]{1,0:T(8,128)(2,1)} %reshape.27, s32[64,32]{0,1:T(8,128)S(1)} %convert_reduce_fusion), kind=kOutput, calls=%fused_computation.25 | convolution fusion | flops 150996992 | bytes 11804672 | tf_op jit(solution)/shard_map/dot_general | solution.py:41
  37.6 164.9 %reduce-scatter.2.cloned.1.call-done = f32[8,36864]{1,0:T(8,128)} async-done(((f32[64,36864]{1,0:T(8,128)}), f32[8,36864]{1,0:T(8,128)}) %reduce-scatter.2.cloned.1.call-update) | async-done | bytes 1179664 | tf_op jit(solution)/shard_map/reduce_scatter | solution.py:40
  202.5 3.1 all_gather_reshape.3
  205.7 2.9 reshape.28
  208.7 0.2 all-gather.6.cloned.1.call-start
  208.9 42.4 %all-gather.4.cloned.1.call-done = f32[4,8,192,192]{3,2,1,0:T(8,128)} async-done(((f32[1,8,192,192]{3,2,1,0:T(8,128)}), f32[4,8,192,192]{3,2,1,0:T(8,128)}) %all-gather.4.cloned.1.call-update) | async-done | bytes 4718608 | tf_op jit(solution)/shard_map/all_gather | solution.py:46
  251.3 4.5 reduce_sum.19
  255.8 2.6 convolution_convert_fusion
  258.4 0.1 copy.24
  258.5 0.1 reshape.32
  258.6 6.1 %reshape.24 = bf16[32,192,192]{2,1,0:T(8,128)(2,1)} reshape(bf16[32,36864]{1,0:T(8,128)(2,1)} %param.10) | data formatting | bytes 4718592 | tf_op jit(solution)/shard_map/reshape | solution.py:16
  264.8 87.3 %all-gather.8.cloned.1.call-done = bf16[64,192,192]{2,1,0:T(8,128)(2,1)} async-done(((bf16[8,192,192]{2,1,0:T(8,128)(2,1)}), bf16[64,192,192]{2,1,0:T(8,128)(2,1)}) %all-gather.8.cloned.1.call-update) | async-done | bytes 4718608 | tf_op jit(solution)/shard_map/all_gather | solution.py:55
  352.1 6.3 %gather_fusion.1 = bf16[64,192,192]{2,1,0:T(8,128)(2,1)} fusion(bf16[64,192,192]{2,1,0:T(8,128)(2,1)} %all-gather.8.cloned.1.call-done, s32[1024]{0:T(1024)S(1)} %pad_clamp_fusion), kind=kCustom, calls=%fused_computation.1 | custom fusion | bytes 9437440 | tf_op jit(solution)/shard_map/gather | solution.py:57
  358.4 92.5 %all-gather.6.cloned.1.call-done = bf16[64,192,192]{2,1,0:T(8,128)(2,1)} async-done(((bf16[8,192,192]{2,1,0:T(8,128)(2,1)}), bf16[64,192,192]{2,1,0:T(8,128)(2,1)}) %all-gather.6.cloned.1.call-update) | async-done | bytes 4718608 | tf_op jit(solution)/shard_map/all_gather | solution.py:54
  451.0 6.3 %gather_fusion = bf16[64,192,192]{2,1,0:T(8,128)(2,1)} fusion(bf16[64,192,192]{2,1,0:T(8,128)(2,1)} %all-gather.6.cloned.1.call-done, s32[1024]{0:T(1024)S(1)} %pad_clamp_fusion), kind=kCustom, calls=%fused_computation | custom fusion | bytes 9437440 | tf_op jit(solution)/shard_map/gather | solution.py:58
  457.3 9.7 %copy.25 = f32[64,192,192]{1,2,0:T(8,128)} copy(bf16[64,192,192]{2,1,0:T(8,128)(2,1)} %gather_fusion) | data formatting | bytes 14155776 | tf_op jit(solution)/shard_map/convert_element_type | solution.py:62
  467.0 11.2 %fusion = bf16[32,2,192,192]{2,3,1,0:T(8,128)(2,1)} fusion(f32[32,2,192,192]{2,3,1,0:T(8,128)} %bitcast.27, bf16[32,2,192,192]{3,2,1,0:T(8,128)(2,1)} %bitcast.28, bf16[32,192,192]{2,1,0:T(8,128)(2,1)} %fusion.19), kind=kOutput, calls=%fused_computation.3 | convolution fusion | flops 915406848 | bytes 21233664 | tf_op jit(solution)/shard_map/pab,pebc->peac/dot_general | solution.py:59
  478.2 7.5 %fusion.9 = f32[32,192,192]{2,1,0:T(8,128)} fusion(bf16[32,192,192]{2,1,0:T(8,128)(2,1)S(1)} %reshape.26, bf16[32,2,192,192]{2,3,1,0:T(8,128)(2,1)} %fusion), kind=kOutput, calls=%fused_computation.15 | convolution fusion | flops 911867904 | bytes 15728640 | tf_op jit(solution)/shard_map/pab,pbc->pac/dot_general | solution.py:71
  485.7 7.9 %select_convert_fusion = bf16[32,192,192]{2,1,0:T(8,128)(2,1)S(1)} fusion(f32[32,192,192]{2,1,0:T(8,128)} %fusion.9, bf16[32,192,192]{2,1,0:T(8,128)(2,1)} %reshape.24, s32[32]{0:T(128)S(1)} %add_multiply_fusion, bf16[32,192,192]{2,1,0:T(8,128)(2,1)} %reshape.25), kind=kOutput, calls=%fused_computation.4 | convolution fusion | flops 467140608 | bytes 11796608 | tf_op jit(solution)/shard_map/pab,pbc->pac/dot_general | solution.py:34
  493.6 4.2 reshape.29
  (15 shorter events, 0.2 us)
Async XLA Ops:
  6.5 196.0 %reduce-scatter.2.cloned.1.call-start = ((), (), s32[]{:S(2)}) async-start(), calls=%async_computation.1 | async-start | bytes 10616832 | tf_op jit(solution)/shard_map/reduce_scatter | solution.py:40
  12.6 5.0 copy-start.1
  24.6 6.2 %copy-start = (s32[32,2]{0,1:T(2,128)S(1)}, s32[32,2]{0,1:T(2,128)}, u32[]{:S(2)}) copy-start(s32[32,2]{0,1:T(2,128)} %param.6) | copy-start | bytes 772
  37.5 213.7 %all-gather.4.cloned.1.call-start = ((), (), s32[]{:S(2)}) async-start(), calls=%async_computation.2 | async-start | bytes 7864320 | tf_op jit(solution)/shard_map/all_gather | solution.py:46
  205.7 146.4 %all-gather.8.cloned.1.call-start = ((), (), s32[]{:S(2)}) async-start(), calls=%async_computation.4 | async-start | bytes 7077888 | tf_op jit(solution)/shard_map/all_gather | solution.py:55
  208.7 242.3 %all-gather.6.cloned.1.call-start = ((), (), s32[]{:S(2)}) async-start(), calls=%async_computation.3 | async-start | bytes 7077888 | tf_op jit(solution)/shard_map/all_gather | solution.py:54
Sparse Core Ops, SparseCore 0:
  37.7 164.8 reduce-scatter.1
  205.8 45.4 all-gather.3
  253.4 98.6 all-gather.7
  354.1 96.8 all-gather.5
